TPU v7x, 32 devices: a whole 2x2x4 slice. The times are simulated.
32 devices in a mesh: gx: 2 (over x), gy: 4 (over y, core), gz: 4 (over z).
Axes of the slice: x: 2, y: 2, z: 4, core: 2. Of those that a mesh axis runs over, the one named last changes fastest.
Arguments:
- vorticity: float32 [3, 16, 64, 512], P(None, 'gx', 'gy', 'gz'), may hold values from -6 to 6
- velocity: float32 [3, 16, 64, 512], P(None, 'gx', 'gy', 'gz'), may hold values from -1 to 1
Outputs:
- vorticity_out: float32 [3, 16, 64, 512], P(None, 'gx', 'gy', 'gz')
All inputs are finite; a program needn't handle non-finite values.
Results may differ from a plain program's by a relative error of at most 0.0003.
Values sent between devices are 32-bit elements; how exact they have to be, the bound alone decides.
A program may use at most 64 MiB of HBM per device.

v0:
```python
import jax
import jax.numpy as jnp
from jax import lax
from jax.sharding import PartitionSpec as P

SUBSTEPS = 2


time_step = 0.5


def extended(cells, sides, width):
    for axis, dim in sides:
        count = lax.axis_size(axis)
        head = lax.slice_in_dim(cells, 0, width, axis=dim)
        tail = lax.slice_in_dim(cells, cells.shape[dim] - width, cells.shape[dim], axis=dim)
        cells = jnp.concatenate(
            [
                lax.ppermute(tail, axis, [(i, (i + 1) % count) for i in range(count)]),
                cells,
                lax.ppermute(head, axis, [((i + 1) % count, i) for i in range(count)]),
            ],
            axis=dim,
        )
    return cells


def kernel(distance):
    magnitude = jnp.abs(distance)
    near = 1.0 - 2.5 * magnitude * magnitude + 1.5 * magnitude * magnitude * magnitude
    far = 0.5 * (2.0 - magnitude) * (2.0 - magnitude) * (1.0 - magnitude)
    return jnp.where(magnitude < 1.0, near, jnp.where(magnitude < 2.0, far, 0.0))


def spread(current, displace, along):
    widened = None
    for offset in range(-2, 3):
        weighted = kernel(offset - displace) * current
        widths = [(0, 0), (0, 0), (0, 0), (0, 0)]
        widths[along] = (2 + offset, 2 - offset)
        padded = jnp.pad(weighted, widths)
        widened = padded if widened is None else widened + padded
    return widened


def derive(reach, along, length):

    def window(first):
        return lax.slice_in_dim(reach, first, first + length, axis=along)

    return (8.0 * (window(3) - window(1)) - (window(4) - window(0))) / 12.0


def add_edges(interior, leading, trailing, along, length):
    filler_shape = list(interior.shape)
    filler_shape[along] = length - 4
    filler = jnp.zeros(filler_shape, jnp.float32)
    return interior + jnp.concatenate([leading, filler, trailing], axis=along)


def settle(widened, received, along, length):
    interior = lax.slice_in_dim(widened, 2, length + 2, axis=along)
    leading = lax.slice_in_dim(received, 0, 2, axis=along)
    trailing = lax.slice_in_dim(received, 6, 8, axis=along)
    return add_edges(interior, leading, trailing, along, length)


def carry_later(border_strip, along):
    if along == 1:
        return extended(border_strip, (("gx", 1),), 2)
    if along == 2:
        return extended(border_strip, (("gy", 2),), 2)
    return extended(border_strip, (("gz", 3),), 2)


def carry_joined(border_strip, along):
    if along == 1:
        return extended(border_strip, (("gx", 1),), 2)
    if along == 2:
        return extended(border_strip, (("gy", 2),), 2)
    return extended(border_strip, (("gz", 3),), 2)


def edge_layers(widened, along, length):
    return jnp.concatenate(
        [
            lax.slice_in_dim(widened, 0, 2, axis=along),
            lax.slice_in_dim(widened, length + 2, length + 4, axis=along),
        ],
        axis=along,
    )


def local(vorticity, velocity):
    extents = vorticity.shape[1:]
    slopes = [None, None, None]
    current = vorticity
    for substep in range(SUBSTEPS):
        for along in (1, 2, 3):
            length = extents[along - 1]
            widened = spread(current, time_step * velocity[along - 1], along)
            ghosts = edge_layers(widened, along, length)
            if substep == 0:
                border = jnp.concatenate(
                    [
                        lax.slice_in_dim(velocity, 0, 2, axis=along),
                        lax.slice_in_dim(velocity, length - 2, length, axis=along),
                    ],
                    axis=along,
                )
                received = carry_joined(jnp.concatenate([ghosts, border], axis=0), along)
                moving = received[3:]
                reach = jnp.concatenate(
                    [
                        lax.slice_in_dim(moving, 0, 2, axis=along),
                        velocity,
                        lax.slice_in_dim(moving, 6, 8, axis=along),
                    ],
                    axis=along,
                )
                slopes[along - 1] = derive(reach, along, length)
                received = received[:3]
            else:
                received = carry_later(ghosts, along)
            current = settle(widened, received, along, length)
        stretch = current[0] * slopes[0] + current[1] * slopes[1] + current[2] * slopes[2]
        current = current + time_step * stretch
    return current


def solution(mesh):
    placed = (P(None, "gx", "gy", "gz"), P(None, "gx", "gy", "gz"))
    return jax.shard_map(
        local, mesh=mesh, in_specs=placed, out_specs=P(None, "gx", "gy", "gz"), check_vma=False
    )
```

profile of v0, /device:TPU:0, one launch (start us, length us, event | category | flops | bytes accessed | tf_op | source)
XLA Modules:
  0.0 49.6 jit_solution(9465080713706896775)
XLA Ops:
  0.0 0.0 copy-start.1
  0.0 1.5 %fusion.20 = (f32[8,16,128]{2,1,0:T(8,128)S(1)}, f32[8,16,128]{2,1,0:T(8,128)S(1)}, f32[8,16,128]{2,1,0:T(8,128)S(1)}, f32[8,16,128]{2,1,0:T(8,128)S(1)}, f32[8,...) fusion(f32[3,8,16,128]{3,2,1,0:T(8,128)} %param.3), kind=kLoop, calls=%fused_computation.127 | loop fusion | flops 4472832 | bytes 1179648 | tf_op jit(solution)/shard_map/mul | solution.py:38
  1.5 0.0 copy-done.1
  1.5 0.0 copy-start
  1.5 0.1 broadcast_multiply_fusion.25
  1.7 0.8 %copy-done = f32[3,8,16,128]{3,2,1,0:T(8,128)S(1)} copy-done((f32[3,8,16,128]{3,2,1,0:T(8,128)S(1)}, f32[3,8,16,128]{3,2,1,0:T(8,128)}, u32[]{:S(2)}) %copy-start) | copy-done | bytes 196632
  2.5 3.0 %collective-permute-start = (f32[6,2,16,128]{3,2,1,0:T(8,128)S(1)}, f32[6,2,16,128]{3,2,1,0:T(8,128)S(1)}, u32[]{:S(2)}, u32[]{:S(2)}) collective-permute-start(f32[6,2,16,128]{3,2,1,0:T(8,128)S(1)} %get-tuple-element.69), channel_id=1, source_target_pairs={{0,16},{16,0},{1,17},{17,1},{2,18},{18,2},{3,19},{19,3},{4,20},{20... | collective-permute-start | bytes 294920 | tf_op jit(solution)/shard_map/ppermute | solution.py:19
  5.6 0.1 collective-permute-start.1
  5.7 0.1 fusion.118
  5.8 0.1 pad_add_fusion.5
  5.9 0.1 pad.162.clone
  5.9 0.1 pad.155.clone
  6.0 0.1 pad.169.clone
  6.1 0.2 copy.82
  6.3 0.2 copy.83
  6.6 2.4 %collective-permute-done = f32[6,2,16,128]{3,2,1,0:T(8,128)S(1)} collective-permute-done((f32[6,2,16,128]{3,2,1,0:T(8,128)S(1)}, f32[6,2,16,128]{3,2,1,0:T(8,128)S(1)}, u32[]{:S(2)}, u32[]{:S(2)}) %collective-permute-start) | collective-permute-done | bytes 98336 | tf_op jit(solution)/shard_map/ppermute | solution.py:19
  9.0 1.5 %collective-permute-done.1 = f32[6,2,16,128]{3,2,1,0:T(8,128)S(1)} collective-permute-done((f32[6,2,16,128]{3,2,1,0:T(8,128)S(1)}, f32[6,2,16,128]{3,2,1,0:T(8,128)S(1)}, u32[]{:S(2)}, u32[]{:S(2)}) %collective-permute-start.1) | collective-permute-done | bytes 98336 | tf_op jit(solution)/shard_map/ppermute | solution.py:21
  10.5 0.1 broadcast_multiply_fusion.27
  10.6 0.1 broadcast_multiply_fusion.15
  10.8 0.1 collective-permute-start.2
  10.8 0.1 pad_add_fusion.4
  11.0 1.8 %collective-permute-start.3 = (f32[6,8,2,128]{3,1,2,0:T(8,128)S(1)}, f32[6,8,2,128]{3,1,2,0:T(8,128)S(1)}, u32[]{:S(2)}, u32[]{:S(2)}) collective-permute-start(f32[6,8,2,128]{3,1,2,0:T(8,128)S(1)} %get-tuple-element.87), channel_id=1, source_target_pairs={{4,0},{8,4},{12,8},{0,12},{5,1},{9,5},{13,9},{1,13},{6,2},{10,6},{... | collective-permute-start | bytes 147464 | tf_op jit(solution)/shard_map/ppermute | solution.py:21
  12.7 1.6 %collective-permute-done.2 = f32[6,8,2,128]{3,1,2,0:T(8,128)S(1)} collective-permute-done((f32[6,8,2,128]{3,1,2,0:T(8,128)S(1)}, f32[6,8,2,128]{3,1,2,0:T(8,128)S(1)}, u32[]{:S(2)}, u32[]{:S(2)}) %collective-permute-start.2) | collective-permute-done | bytes 49184 | tf_op jit(solution)/shard_map/ppermute | solution.py:19
  14.4 0.1 collective-permute-done.3
  14.5 0.1 broadcast_multiply_fusion.1
  14.6 0.1 broadcast_multiply_fusion.29
  14.8 0.5 pad_add_fusion.1
  15.2 0.1 fusion.117
  15.4 0.2 copy.66
  15.5 0.2 copy.67
  15.8 4.0 %collective-permute-start.5 = (f32[6,8,16,2]{2,1,3,0:T(8,128)S(1)}, f32[6,8,16,2]{2,1,3,0:T(8,128)S(1)}, u32[]{:S(2)}, u32[]{:S(2)}) collective-permute-start(f32[6,8,16,2]{2,1,3,0:T(8,128)S(1)} %get-tuple-element.85), channel_id=1, source_target_pairs={{1,0},{2,1},{3,2},{0,3},{5,4},{6,5},{7,6},{4,7},{9,8},{10,9},{11,1... | collective-permute-start | bytes 18440 | tf_op jit(solution)/shard_map/ppermute | solution.py:21
  19.9 0.1 collective-permute-start.4
  19.9 1.6 %collective-permute-done.5 = f32[6,8,16,2]{2,1,3,0:T(8,128)S(1)} collective-permute-done((f32[6,8,16,2]{2,1,3,0:T(8,128)S(1)}, f32[6,8,16,2]{2,1,3,0:T(8,128)S(1)}, u32[]{:S(2)}, u32[]{:S(2)}) %collective-permute-start.5) | collective-permute-done | bytes 6176 | tf_op jit(solution)/shard_map/ppermute | solution.py:21
  21.6 0.2 copy.74
  21.8 4.1 %collective-permute-done.4 = f32[6,8,16,2]{2,1,3,0:T(8,128)S(1)} collective-permute-done((f32[6,8,16,2]{2,1,3,0:T(8,128)S(1)}, f32[6,8,16,2]{2,1,3,0:T(8,128)S(1)}, u32[]{:S(2)}, u32[]{:S(2)}) %collective-permute-start.4) | collective-permute-done | bytes 6176 | tf_op jit(solution)/shard_map/ppermute | solution.py:19
  25.9 0.2 copy.75
  26.1 0.2 copy.71
  26.4 0.2 copy.70
  26.6 0.2 slice_add_fusion.3
  26.8 0.4 broadcast_multiply_fusion.24
  27.2 0.1 broadcast_multiply_fusion.22
  27.3 1.5 %collective-permute-start.6 = (f32[3,2,16,128]{3,2,1,0:T(8,128)S(1)}, f32[3,2,16,128]{3,2,1,0:T(8,128)S(1)}, u32[]{:S(2)}, u32[]{:S(2)}) collective-permute-start(f32[3,2,16,128]{3,2,1,0:T(8,128)S(1)} %get-tuple-element.16), channel_id=1, source_target_pairs={{0,16},{16,0},{1,17},{17,1},{2,18},{18,2},{3,19},{19,3},{4,20},{20... | collective-permute-start | bytes 147464 | tf_op jit(solution)/shard_map/ppermute | solution.py:19
  28.8 0.6 %collective-permute-start.7 = (f32[3,2,16,128]{3,2,1,0:T(8,128)S(1)}, f32[3,2,16,128]{3,2,1,0:T(8,128)S(1)}, u32[]{:S(2)}, u32[]{:S(2)}) collective-permute-start(f32[3,2,16,128]{3,2,1,0:T(8,128)S(1)} %get-tuple-element.17), channel_id=1, source_target_pairs={{16,0},{0,16},{17,1},{1,17},{18,2},{2,18},{19,3},{3,19},{20,4},{4,... | collective-permute-start | bytes 147464 | tf_op jit(solution)/shard_map/ppermute | solution.py:21
  29.4 0.1 pad_add_fusion.3
  29.5 2.1 %collective-permute-done.6 = f32[3,2,16,128]{3,2,1,0:T(8,128)S(1)} collective-permute-done((f32[3,2,16,128]{3,2,1,0:T(8,128)S(1)}, f32[3,2,16,128]{3,2,1,0:T(8,128)S(1)}, u32[]{:S(2)}, u32[]{:S(2)}) %collective-permute-start.6) | collective-permute-done | bytes 49184 | tf_op jit(solution)/shard_map/ppermute | solution.py:19
  31.6 1.3 %collective-permute-done.7 = f32[3,2,16,128]{3,2,1,0:T(8,128)S(1)} collective-permute-done((f32[3,2,16,128]{3,2,1,0:T(8,128)S(1)}, f32[3,2,16,128]{3,2,1,0:T(8,128)S(1)}, u32[]{:S(2)}, u32[]{:S(2)}) %collective-permute-start.7) | collective-permute-done | bytes 49184 | tf_op jit(solution)/shard_map/ppermute | solution.py:21
  32.9 0.1 broadcast_multiply_fusion.26
  33.0 0.1 broadcast_multiply_fusion.14
  33.1 0.1 collective-permute-start.9
  33.2 0.5 %collective-permute-start.8 = (f32[3,8,2,128]{3,1,2,0:T(8,128)S(1)}, f32[3,8,2,128]{3,1,2,0:T(8,128)S(1)}, u32[]{:S(2)}, u32[]{:S(2)}) collective-permute-start(f32[3,8,2,128]{3,1,2,0:T(8,128)S(1)} %copy.76), channel_id=1, source_target_pairs={{0,4},{4,8},{8,12},{12,0},{1,5},{5,9},{9,13},{13,1},{2,6},{6,10},{... | collective-permute-start | bytes 73736 | tf_op jit(solution)/shard_map/ppermute | solution.py:19
  33.7 0.1 pad_add_fusion.2
  33.8 0.9 %collective-permute-done.9 = f32[3,8,2,128]{3,1,2,0:T(8,128)S(1)} collective-permute-done((f32[3,8,2,128]{3,1,2,0:T(8,128)S(1)}, f32[3,8,2,128]{3,1,2,0:T(8,128)S(1)}, u32[]{:S(2)}, u32[]{:S(2)}) %collective-permute-start.9) | collective-permute-done | bytes 24608 | tf_op jit(solution)/shard_map/ppermute | solution.py:21
  34.7 1.9 %collective-permute-done.8 = f32[3,8,2,128]{3,1,2,0:T(8,128)S(1)} collective-permute-done((f32[3,8,2,128]{3,1,2,0:T(8,128)S(1)}, f32[3,8,2,128]{3,1,2,0:T(8,128)S(1)}, u32[]{:S(2)}, u32[]{:S(2)}) %collective-permute-start.8) | collective-permute-done | bytes 24608 | tf_op jit(solution)/shard_map/ppermute | solution.py:19
  36.7 0.1 broadcast_multiply_fusion
  36.8 0.1 broadcast_multiply_fusion.28
  36.9 0.5 pad_add_fusion
  37.4 0.1 fusion.116
  37.5 0.1 collective-permute-start.10
  37.6 3.8 %collective-permute-start.11 = (f32[3,8,16,2]{3,2,1,0:T(8,128)S(1)}, f32[3,8,16,2]{3,2,1,0:T(8,128)S(1)}, u32[]{:S(2)}, u32[]{:S(2)}) collective-permute-start(f32[3,8,16,2]{3,2,1,0:T(8,128)S(1)} %get-tuple-element.23), channel_id=1, source_target_pairs={{1,0},{2,1},{3,2},{0,3},{5,4},{6,5},{7,6},{4,7},{9,8},{10,9},{11,1... | collective-permute-start | bytes 9224 | tf_op jit(solution)/shard_map/ppermute | solution.py:21
  41.4 5.8 %collective-permute-done.10 = f32[3,8,16,2]{3,2,1,0:T(8,128)S(1)} collective-permute-done((f32[3,8,16,2]{3,2,1,0:T(8,128)S(1)}, f32[3,8,16,2]{3,2,1,0:T(8,128)S(1)}, u32[]{:S(2)}, u32[]{:S(2)}) %collective-permute-start.10) | collective-permute-done | bytes 3104 | tf_op jit(solution)/shard_map/ppermute | solution.py:19
  47.2 1.5 %collective-permute-done.11 = f32[3,8,16,2]{3,2,1,0:T(8,128)S(1)} collective-permute-done((f32[3,8,16,2]{3,2,1,0:T(8,128)S(1)}, f32[3,8,16,2]{3,2,1,0:T(8,128)S(1)}, u32[]{:S(2)}, u32[]{:S(2)}) %collective-permute-start.11) | collective-permute-done | bytes 3104 | tf_op jit(solution)/shard_map/ppermute | solution.py:21
  48.7 0.2 slice_add_fusion
  48.9 0.8 %multiply_add_fusion = f32[3,8,16,128]{3,2,1,0:T(8,128)} fusion(f32[3,8,16,128]{3,2,1,0:T(8,128)S(1)} %slice_add_fusion, f32[3,8,16,128]{3,2,1,0:T(8,128)S(1)} %get-tuple-element.11, f32[3,8,16,128]{3,2,1,0:T(8,128)S(1)} %get-tuple-element.10, f32[3,8,16,128]{3,2,1,0:T(8,128)S(1)} %get-tuple-element.9, f32[8,16,128]{2,1,0:T(8,128)S(1)} %get-tuple-element.35, ...), kind=kLoop, calls=%fused_computation.45 | loop fusion | flops 344064 | bytes 1179648 | tf_op jit(solution)/shard_map/add | solution.py:127
  (35 shorter events, 0.5 us)
Async XLA Ops:
  0.0 1.5 %copy-start.1 = (f32[3,8,16,128]{3,2,1,0:T(8,128)S(1)}, f32[3,8,16,128]{3,2,1,0:T(8,128)}, u32[]{:S(2)}) copy-start(f32[3,8,16,128]{3,2,1,0:T(8,128)} %param.2) | copy-start | bytes 589828
  1.5 0.9 %copy-start = (f32[3,8,16,128]{3,2,1,0:T(8,128)S(1)}, f32[3,8,16,128]{3,2,1,0:T(8,128)}, u32[]{:S(2)}) copy-start(f32[3,8,16,128]{3,2,1,0:T(8,128)} %param.3) | copy-start | bytes 589828
  2.5 6.5 %collective-permute-start = (f32[6,2,16,128]{3,2,1,0:T(8,128)S(1)}, f32[6,2,16,128]{3,2,1,0:T(8,128)S(1)}, u32[]{:S(2)}, u32[]{:S(2)}) collective-permute-start(f32[6,2,16,128]{3,2,1,0:T(8,128)S(1)} %get-tuple-element.69), channel_id=1, source_target_pairs={{0,16},{16,0},{1,17},{17,1},{2,18},{18,2},{3,19},{19,3},{4,20},{20... | collective-permute-start | bytes 294920 | tf_op jit(solution)/shard_map/ppermute | solution.py:19
  5.6 4.9 %collective-permute-start.1 = (f32[6,2,16,128]{3,2,1,0:T(8,128)S(1)}, f32[6,2,16,128]{3,2,1,0:T(8,128)S(1)}, u32[]{:S(2)}, u32[]{:S(2)}) collective-permute-start(f32[6,2,16,128]{3,2,1,0:T(8,128)S(1)} %get-tuple-element.70), channel_id=1, source_target_pairs={{16,0},{0,16},{17,1},{1,17},{18,2},{2,18},{19,3},{3,19},{20,4},{4,... | collective-permute-start | bytes 294920 | tf_op jit(solution)/shard_map/ppermute | solution.py:21
  10.8 3.6 %collective-permute-start.2 = (f32[6,8,2,128]{3,1,2,0:T(8,128)S(1)}, f32[6,8,2,128]{3,1,2,0:T(8,128)S(1)}, u32[]{:S(2)}, u32[]{:S(2)}) collective-permute-start(f32[6,8,2,128]{3,1,2,0:T(8,128)S(1)} %get-tuple-element.86), channel_id=1, source_target_pairs={{0,4},{4,8},{8,12},{12,0},{1,5},{5,9},{9,13},{13,1},{2,6},{6,10},{... | collective-permute-start | bytes 147464 | tf_op jit(solution)/shard_map/ppermute | solution.py:19
  11.0 3.5 %collective-permute-start.3 = (f32[6,8,2,128]{3,1,2,0:T(8,128)S(1)}, f32[6,8,2,128]{3,1,2,0:T(8,128)S(1)}, u32[]{:S(2)}, u32[]{:S(2)}) collective-permute-start(f32[6,8,2,128]{3,1,2,0:T(8,128)S(1)} %get-tuple-element.87), channel_id=1, source_target_pairs={{4,0},{8,4},{12,8},{0,12},{5,1},{9,5},{13,9},{1,13},{6,2},{10,6},{... | collective-permute-start | bytes 147464 | tf_op jit(solution)/shard_map/ppermute | solution.py:21
  15.8 5.7 %collective-permute-start.5 = (f32[6,8,16,2]{2,1,3,0:T(8,128)S(1)}, f32[6,8,16,2]{2,1,3,0:T(8,128)S(1)}, u32[]{:S(2)}, u32[]{:S(2)}) collective-permute-start(f32[6,8,16,2]{2,1,3,0:T(8,128)S(1)} %get-tuple-element.85), channel_id=1, source_target_pairs={{1,0},{2,1},{3,2},{0,3},{5,4},{6,5},{7,6},{4,7},{9,8},{10,9},{11,1... | collective-permute-start | bytes 18440 | tf_op jit(solution)/shard_map/ppermute | solution.py:21
  19.9 6.1 %collective-permute-start.4 = (f32[6,8,16,2]{2,1,3,0:T(8,128)S(1)}, f32[6,8,16,2]{2,1,3,0:T(8,128)S(1)}, u32[]{:S(2)}, u32[]{:S(2)}) collective-permute-start(f32[6,8,16,2]{2,1,3,0:T(8,128)S(1)} %get-tuple-element.84), channel_id=1, source_target_pairs={{0,1},{1,2},{2,3},{3,0},{4,5},{5,6},{6,7},{7,4},{8,9},{9,10},{10,1... | collective-permute-start | bytes 18440 | tf_op jit(solution)/shard_map/ppermute | solution.py:19
  27.3 4.3 %collective-permute-start.6 = (f32[3,2,16,128]{3,2,1,0:T(8,128)S(1)}, f32[3,2,16,128]{3,2,1,0:T(8,128)S(1)}, u32[]{:S(2)}, u32[]{:S(2)}) collective-permute-start(f32[3,2,16,128]{3,2,1,0:T(8,128)S(1)} %get-tuple-element.16), channel_id=1, source_target_pairs={{0,16},{16,0},{1,17},{17,1},{2,18},{18,2},{3,19},{19,3},{4,20},{20... | collective-permute-start | bytes 147464 | tf_op jit(solution)/shard_map/ppermute | solution.py:19
  28.8 4.1 %collective-permute-start.7 = (f32[3,2,16,128]{3,2,1,0:T(8,128)S(1)}, f32[3,2,16,128]{3,2,1,0:T(8,128)S(1)}, u32[]{:S(2)}, u32[]{:S(2)}) collective-permute-start(f32[3,2,16,128]{3,2,1,0:T(8,128)S(1)} %get-tuple-element.17), channel_id=1, source_target_pairs={{16,0},{0,16},{17,1},{1,17},{18,2},{2,18},{19,3},{3,19},{20,4},{4,... | collective-permute-start | bytes 147464 | tf_op jit(solution)/shard_map/ppermute | solution.py:21
  33.1 1.6 %collective-permute-start.9 = (f32[3,8,2,128]{3,1,2,0:T(8,128)S(1)}, f32[3,8,2,128]{3,1,2,0:T(8,128)S(1)}, u32[]{:S(2)}, u32[]{:S(2)}) collective-permute-start(f32[3,8,2,128]{3,1,2,0:T(8,128)S(1)} %copy.77), channel_id=1, source_target_pairs={{4,0},{8,4},{12,8},{0,12},{5,1},{9,5},{13,9},{1,13},{6,2},{10,6},{... | collective-permute-start | bytes 73736 | tf_op jit(solution)/shard_map/ppermute | solution.py:21
  33.2 3.5 %collective-permute-start.8 = (f32[3,8,2,128]{3,1,2,0:T(8,128)S(1)}, f32[3,8,2,128]{3,1,2,0:T(8,128)S(1)}, u32[]{:S(2)}, u32[]{:S(2)}) collective-permute-start(f32[3,8,2,128]{3,1,2,0:T(8,128)S(1)} %copy.76), channel_id=1, source_target_pairs={{0,4},{4,8},{8,12},{12,0},{1,5},{5,9},{9,13},{13,1},{2,6},{6,10},{... | collective-permute-start | bytes 73736 | tf_op jit(solution)/shard_map/ppermute | solution.py:19
  37.5 9.7 %collective-permute-start.10 = (f32[3,8,16,2]{3,2,1,0:T(8,128)S(1)}, f32[3,8,16,2]{3,2,1,0:T(8,128)S(1)}, u32[]{:S(2)}, u32[]{:S(2)}) collective-permute-start(f32[3,8,16,2]{3,2,1,0:T(8,128)S(1)} %get-tuple-element.22), channel_id=1, source_target_pairs={{0,1},{1,2},{2,3},{3,0},{4,5},{5,6},{6,7},{7,4},{8,9},{9,10},{10,1... | collective-permute-start | bytes 9224 | tf_op jit(solution)/shard_map/ppermute | solution.py:19
  37.6 11.1 %collective-permute-start.11 = (f32[3,8,16,2]{3,2,1,0:T(8,128)S(1)}, f32[3,8,16,2]{3,2,1,0:T(8,128)S(1)}, u32[]{:S(2)}, u32[]{:S(2)}) collective-permute-start(f32[3,8,16,2]{3,2,1,0:T(8,128)S(1)} %get-tuple-element.23), channel_id=1, source_target_pairs={{1,0},{2,1},{3,2},{0,3},{5,4},{6,5},{7,6},{4,7},{9,8},{10,9},{11,1... | collective-permute-start | bytes 9224 | tf_op jit(solution)/shard_map/ppermute | solution.py:21
where the time goes:
time: 49.8 us; the launch traced here: 49.6 us
  waiting for transfers between devices  24.9 us (50%)
  starting transfers between devices  15.5 us (31%)
  other arithmetic  5.56 us (11%)
  local copies, waits for them, and re-layouts  3.31 us (7%)
    ppermute x6, waiting for transfers between devices, extended(): lax.ppermute(tail, axis, [(i, (i + 1) % count) for i in range(count)])  18 us
    ppermute x6, starting transfers between devices, extended(): lax.ppermute(head, axis, [((i + 1) % count, i) for i in range(count)])  10.3 us
    ppermute x6, waiting for transfers between devices, extended(): lax.ppermute(head, axis, [((i + 1) % count, i) for i in range(count)])  6.89 us
    ppermute x6, starting transfers between devices, extended(): lax.ppermute(tail, axis, [(i, (i + 1) % count) for i in range(count)])  5.18 us
    mul x12, other arithmetic, spread(): weighted = kernel(offset - displace) * current  2.93 us
    add x6, other arithmetic, spread(): widened = padded if widened is None else widened + padded  1.33 us
    unnamed x9, local copies, waits for them, and re-layouts  1.27 us
  transfers between devices with their start and end apart: 12, of which 12 were waited for; matrix products, arithmetic and copies ran while one was open for 3% of the time, Pallas kernels for 0%

commit v1 on v0

v1 whole, which is shorter than its diff:
```python
import functools

import jax
import jax.numpy as jnp
from jax import lax
from jax.experimental import pallas as pl
from jax.experimental.pallas import tpu as pltpu
from jax.sharding import PartitionSpec as P

SUBSTEPS = 2
TIME_STEP = 0.5
AXES = ("gx", "gy", "gz")
MESH = pl.DeviceIdType.MESH


def roll(values, shift, axis):
    return pltpu.roll(values, shift % values.shape[axis], axis)


def weights(velocity):
    d = TIME_STEP * velocity
    s = jnp.abs(d)
    t = 1.0 - s
    positive = d > 0.0
    centre = 1.0 + s * s * (1.5 * s - 2.5)
    toward = 1.0 + t * t * (1.5 * t - 2.5)
    away = -0.5 * s * t * t
    beyond = -0.5 * s * s * t
    return (
        jnp.where(positive, 0.0, beyond),
        jnp.where(positive, away, toward),
        centre,
        jnp.where(positive, toward, away),
        jnp.where(positive, beyond, 0.0),
    )


def body(
    sizes, vort, vel, out, wgt, slope, cur, sx, rx, sy, ry, sz, rz, rvx, svy, rvy, svz, rvz,
    send_sem, recv_sem,
):
    _, X, Y, Z = vort.shape
    here = [lax.axis_index(a) for a in AXES]

    def neighbour(k, side):
        n = sizes[k]
        moved = lax.rem(here[k] + (1 if side else n - 1), n)
        return tuple(moved if j == k else here[j] for j in range(3))

    def push(src, dst, index, k, side):
        copy = pltpu.make_async_remote_copy(
            src_ref=src, dst_ref=dst, send_sem=send_sem.at[index], recv_sem=recv_sem.at[index],
            device_id=neighbour(k, side), device_id_type=MESH,
        )
        copy.start()
        return copy

    barrier = pltpu.get_barrier_semaphore()
    for k in range(3):
        for side in range(2):
            pl.semaphore_signal(barrier, inc=1, device_id=neighbour(k, side), device_id_type=MESH)

    lane = lax.broadcasted_iota(jnp.int32, (8, Z), 1)
    lane3 = lax.broadcasted_iota(jnp.int32, (X, Y, Z), 2)
    row3 = lax.broadcasted_iota(jnp.int32, (X, Y, Z), 1)
    slabs = [(c, x, y) for c in range(3) for x in range(X) for y in range(0, Y, 8)]
    per = Z // 4

    def pack(edges, target):
        for m in range(0, len(slabs), per):
            held = jnp.zeros((8, Z), jnp.float32)
            for k, (c, x, y) in enumerate(slabs[m:m + per]):
                moved = roll(edges[c][x, y:y + 8, :], 4 * k + 2, 1)
                held = jnp.where(lane // 4 == k, moved, held)
            target[m // per] = held

    def unpack(low_side, high_side):
        merged = [
            jnp.where(lane % 4 >= 2, low_side[m], high_side[m])
            for m in range(-(-len(slabs) // per))
        ]
        edge = (lane < 2) | (lane >= Z - 2)
        return [
            jnp.where(edge, roll(merged[i // per], -(4 * (i % per) + 2), 1), 0.0)
            for i in range(len(slabs))
        ]

    def spread_x(src, step):
        for c in range(3):
            w = [wgt.at[0, a] for a in range(5)]
            sx[step, 0, c, 0] = w[0][0] * src[c, 0]
            sx[step, 0, c, 1] = w[1][0] * src[c, 0] + w[0][1] * src[c, 1]
            sx[step, 1, c, 0] = w[3][X - 1] * src[c, X - 1] + w[4][X - 2] * src[c, X - 2]
            sx[step, 1, c, 1] = w[4][X - 1] * src[c, X - 1]

    def interior_x(src):
        for c in range(3):
            layers = []
            for x in range(X):
                total = None
                for a in range(-2, 3):
                    if 0 <= x - a < X:
                        term = wgt[0, a + 2, x - a] * src[c, x - a]
                        total = term if total is None else total + term
                layers.append(total)
            for x in range(X):
                yield c, x, layers[x]

    def put_weights(k):
        for a, w in enumerate(weights(vel[k])):
            wgt[k, a] = w

    put_weights(0)
    spread_x(vort, 0)
    pl.semaphore_wait(barrier, 6)
    pending = []
    first = [push(sx.at[0, s], rx.at[0, s], s, 0, s) for s in range(2)]
    for s in range(2):
        svy[s] = vel[:, :, pl.ds((Y - 2) * s, 2), :]
    pack([vel[c] for c in range(3)], svz)
    vy = [push(svy.at[s], rvy.at[s], 14 + s, 1, s) for s in range(2)]
    vz = [push(svz, rvz.at[s], 16 + s, 2, s) for s in range(2)]
    vx = [push(vel.at[:, pl.ds((X - 2) * s, 2)], rvx.at[s], 12 + s, 0, s) for s in range(2)]
    put_weights(1)
    put_weights(2)

    scale = TIME_STEP / 12.0

    def slopes_y():
        for c in range(3):
            v = vel[c]
            near = 8.0 * (roll(v, -1, 1) - roll(v, 1, 1)) - (roll(v, -2, 1) - roll(v, 2, 1))
            slope[1, c] = near * scale
        for cp in vy:
            cp.wait()
        for c in range(3):
            top = vel[c, :, 0:4, :]
            low = rvy[1, c]
            slope[1, c, :, 0:1, :] = scale * (
                8.0 * (top[:, 1:2] - low[:, 1:2]) - (top[:, 2:3] - low[:, 0:1]))
            slope[1, c, :, 1:2, :] = scale * (
                8.0 * (top[:, 2:3] - top[:, 0:1]) - (top[:, 3:4] - low[:, 1:2]))
            end = vel[c, :, Y - 4:Y, :]
            high = rvy[0, c]
            slope[1, c, :, Y - 2:Y - 1, :] = scale * (
                8.0 * (end[:, 3:4] - end[:, 1:2]) - (high[:, 0:1] - end[:, 0:1]))
            slope[1, c, :, Y - 1:Y, :] = scale * (
                8.0 * (high[:, 0:1] - end[:, 2:3]) - (high[:, 1:2] - end[:, 1:2]))

    def slopes_z():
        for cp in vz:
            cp.wait()
        halo = unpack(rvz.at[0], rvz.at[1])
        for i, (c, x, y) in enumerate(slabs):
            v = vel[c, x, y:y + 8, :]
            h = halo[i]

            def at(shift):
                source = roll(v, -shift, 1)
                if shift > 0:
                    return jnp.where(lane >= Z - shift, roll(h, -shift, 1), source)
                return jnp.where(lane < -shift, roll(h, -shift, 1), source)

            slope[2, c, x, y:y + 8, :] = scale * (8.0 * (at(1) - at(-1)) - (at(2) - at(-2)))

    def slopes_x():
        for cp in vx:
            cp.wait()
        for c in range(3):
            def layer(x):
                if x < 0:
                    return rvx[1, c, x + 2]
                if x >= X:
                    return rvx[0, c, x - X]
                return vel[c, x]
            for x in range(X):
                slope[0, c, x] = scale * (
                    8.0 * (layer(x + 1) - layer(x - 1)) - (layer(x + 2) - layer(x - 2)))

    for step in range(SUBSTEPS):
        base = step * 6
        src = vort if step == 0 else cur
        if step > 0:
            spread_x(src, step)
            first = [push(sx.at[step, s], rx.at[step, s], base + s, 0, s) for s in range(2)]
        for c, x, layer in interior_x(src):
            cur[c, x] = layer
        if step == 0:
            slopes_y()
            slopes_z()
        for cp in first:
            cp.wait()
        for c in range(3):
            for x in range(2):
                cur[c, x] += rx[step, 1, c, x]
                cur[c, X - 2 + x] += rx[step, 0, c, x]

        for c in range(3):
            v = cur[c]
            u = [wgt[1, a] * v for a in range(5)]
            keep, go = u[2], None
            for a in (-2, -1, 1, 2):
                moved = roll(u[a + 2], a, 1)
                outside = row3 < a if a > 0 else row3 >= Y + a
                keep = keep + jnp.where(outside, 0.0, moved)
                part = jnp.where(outside, moved, 0.0)
                go = part if go is None else go + part
            cur[c] = keep
            sy[step, 1, c] = go[:, 0:2, :]
            sy[step, 0, c] = go[:, Y - 2:Y, :]
        copies = [push(sy.at[step, s], ry.at[step, s], base + 2 + s, 1, s) for s in range(2)]
        if step == 0:
            slopes_x()
        for cp in copies:
            cp.wait()
        for c in range(3):
            cur[c, :, 0:2, :] += ry[step, 1, c]
            cur[c, :, Y - 2:Y, :] += ry[step, 0, c]

        edges = []
        for c in range(3):
            v = cur[c]
            u = [wgt[2, a] * v for a in range(5)]
            keep, go = u[2], None
            for a in (-2, -1, 1, 2):
                moved = roll(u[a + 2], a, 2)
                outside = lane3 < a if a > 0 else lane3 >= Z + a
                keep = keep + jnp.where(outside, 0.0, moved)
                part = jnp.where(outside, moved, 0.0)
                go = part if go is None else go + part
            cur[c] = keep
            edges.append(go)
        pack(edges, sz.at[step])
        copies = [push(sz.at[step], rz.at[step, s], base + 4 + s, 2, s) for s in range(2)]
        for cp in copies:
            cp.wait()
        halo = unpack(rz.at[step, 1], rz.at[step, 0])
        final = out if step == SUBSTEPS - 1 else cur
        for x in range(X):
            for y in range(0, Y, 8):
                v = [
                    cur[c, x, y:y + 8, :] + halo[slabs.index((c, x, y))]
                    for c in range(3)
                ]
                for i in range(3):
                    total = v[i]
                    for j in range(3):
                        total = total + v[j] * slope[j, i, x, y:y + 8, :]
                    final[i, x, y:y + 8, :] = total


def solution(mesh):
    sizes = [mesh.shape[a] for a in AXES]

    def local(vort, vel):
        _, X, Y, Z = vort.shape
        packs = -(-(3 * X * (Y // 8)) // (Z // 4))
        f32 = jnp.float32
        V = pltpu.VMEM
        S = SUBSTEPS
        return pl.pallas_call(
            functools.partial(body, sizes),
            out_shape=jax.ShapeDtypeStruct(vort.shape, f32),
            in_specs=[pl.BlockSpec(memory_space=pltpu.VMEM)] * 2,
            out_specs=pl.BlockSpec(memory_space=pltpu.VMEM),
            scratch_shapes=[
                V((3, 5, X, Y, Z), f32),
                V((3, 3, X, Y, Z), f32),
                V((3, X, Y, Z), f32),
                V((S, 2, 3, 2, Y, Z), f32),
                V((S, 2, 3, 2, Y, Z), f32),
                V((S, 2, 3, X, 2, Z), f32),
                V((S, 2, 3, X, 2, Z), f32),
                V((S, packs, 8, Z), f32),
                V((S, 2, packs, 8, Z), f32),
                V((2, 3, 2, Y, Z), f32),
                V((2, 3, X, 2, Z), f32),
                V((2, 3, X, 2, Z), f32),
                V((packs, 8, Z), f32),
                V((2, packs, 8, Z), f32),
                pltpu.SemaphoreType.DMA((18,)),
                pltpu.SemaphoreType.DMA((18,)),
            ],
            compiler_params=pltpu.CompilerParams(collective_id=0, has_side_effects=True),
        )(vort, vel)

    placed = P(None, *AXES)
    return jax.shard_map(
        local, mesh=mesh, in_specs=(placed, placed), out_specs=placed, check_vma=False
    )
```

time: 49.8 us -> 29.9 us (0.60)
  Pallas kernels: 0 us -> 28.1 us
  waiting for transfers between devices: 24.9 us -> 0 us
  starting transfers between devices: 15.5 us -> 0 us
  other arithmetic: 5.56 us -> 0 us
  local copies, waits for them, and re-layouts: 3.31 us -> 1.62 us
    pallas_call x0 -> x1, Pallas kernels: none -> 28.1 us  [local(): pl.pallas_call(functools.partial(body, sizes), out_shape=jax.ShapeDtypeSt...]
    ppermute x12 -> x0, waiting for transfers between devices: 24.9 us -> none  [the longest x6 18 us: extended(): lax.ppermute(tail, axis, [(i, (i + 1) % count) for i in range(count)])]
    ppermute x12 -> x0, starting transfers between devices: 15.5 us -> none  [the longest x6 10.3 us: extended(): lax.ppermute(head, axis, [((i + 1) % count, i) for i in range(count)])]
    mul x14 -> x0, other arithmetic: 2.97 us -> none  [the longest x12 2.93 us: spread(): weighted = kernel(offset - displace) * current]
    add x9 -> x0, other arithmetic: 2.42 us -> none  [the longest x6 1.33 us: spread(): widened = padded if widened is None else widened + padded]
    slice x26 -> x0, local copies, waits for them, and re-layouts: 1.75 us -> none  [the longest x4 0.34 us: edge_layers(): lax.slice_in_dim(widened, length + 2, length + 4, axis=along)]
    unnamed x9 -> x1, local copies, waits for them, and re-layouts: 1.27 us -> 1.62 us
  transfers between devices with their start and end apart: 12 -> 0, of which waited for: 12 -> 0; matrix products, arithmetic and copies ran while one was open for 3% -> 0% of each run, Pallas kernels for 0% -> 0%
where the time goes in v1:
time: 29.9 us; the launch traced here: 29.8 us
  Pallas kernels  28.1 us (94%)
  local copies, waits for them, and re-layouts  1.62 us (5%)
    pallas_call x1, Pallas kernels, local(): pl.pallas_call(functools.partial(body, sizes), out_shape=jax.ShapeDtypeSt...  28.1 us
    unnamed x1, local copies, waits for them, and re-layouts  1.62 us

profile of v1, /device:TPU:0, one launch (start us, length us, event | category | flops | bytes accessed | tf_op | source)
XLA Modules:
  0.0 29.8 jit_solution(2979071157916114914)
XLA Ops:
  0.0 28.1 %shard_map.28 = f32[3,8,16,128]{3,2,1,0:T(8,128)} custom-call(f32[3,8,16,128]{3,2,1,0:T(8,128)} %vort.1, f32[3,8,16,128]{3,2,1,0:T(8,128)} %vel.1), custom_call_target="tpu_custom_call" | custom-call | tf_op jit(solution)/shard_map/pallas_call | solution.py:261
  28.1 1.6 %copy.4 = f32[3,8,16,128]{3,2,1,0:T(8,128)} copy(f32[3,8,16,128]{3,2,1,0:T(8,128)} %shard_map.28) | data formatting | bytes 393216

commit v2 on v1

v2 whole, which is shorter than its diff:
```python
import functools

import jax
import jax.numpy as jnp
from jax import lax
from jax.experimental import pallas as pl
from jax.experimental.pallas import tpu as pltpu
from jax.sharding import PartitionSpec as P

SUBSTEPS = 2
TIME_STEP = 0.5
AXES = ("gx", "gy", "gz")
MESH = pl.DeviceIdType.MESH


def roll(values, shift, axis):
    return pltpu.roll(values, shift % values.shape[axis], axis)


def weights(velocity):
    d = TIME_STEP * velocity
    s = jnp.abs(d)
    t = 1.0 - s
    positive = d > 0.0
    centre = 1.0 + s * s * (1.5 * s - 2.5)
    toward = 1.0 + t * t * (1.5 * t - 2.5)
    away = -0.5 * s * t * t
    beyond = -0.5 * s * s * t
    return (
        jnp.where(positive, 0.0, beyond),
        jnp.where(positive, away, toward),
        centre,
        jnp.where(positive, toward, away),
        jnp.where(positive, beyond, 0.0),
    )


def body(
    sizes, vort, vel, out, wgt, slope, cur, sx, rx, sy, ry, sxy, rxy, szi, rzi, szx, rzx,
    rvx, svy, rvy, svz, rvz, wyh, send_sem, recv_sem,
):
    _, X, Y, Z = vort.shape
    here = [lax.axis_index(a) for a in AXES]
    f32 = jnp.float32
    both = (-1, 1)
    three = (-1, 0, 1)
    xdirs = (1,) if sizes[0] == 2 else both
    used = [0]

    def device(offset):
        return tuple(
            h if o == 0 else lax.rem(h + (o if o > 0 else n + o), n)
            for h, o, n in zip(here, offset, sizes)
        )

    def push(src, dst, offset):
        index = used[0]
        used[0] += 1
        copy = pltpu.make_async_remote_copy(
            src_ref=src, dst_ref=dst, send_sem=send_sem.at[index], recv_sem=recv_sem.at[index],
            device_id=device(offset), device_id_type=MESH,
        )
        copy.start()
        return copy

    def done(copies):
        for copy in copies:
            copy.wait()

    barrier = pltpu.get_barrier_semaphore()
    greeted = 0
    for dz in three:
        for dy in three:
            for dx in (0,) + xdirs:
                if dx or dy or dz:
                    pl.semaphore_signal(
                        barrier, inc=1, device_id=device((dx, dy, dz)), device_id_type=MESH)
                    greeted += 1

    lane = lax.broadcasted_iota(jnp.int32, (Y, Z), 1)
    lane3 = lax.broadcasted_iota(jnp.int32, (X, Y, Z), 2)
    row3 = lax.broadcasted_iota(jnp.int32, (X, Y, Z), 1)
    edge = (lane < 2) | (lane >= Z - 2)

    def pack(entries):
        held = jnp.zeros((Y, Z), f32)
        for k, values in entries:
            held = jnp.where(lane // 4 == k, roll(values, 4 * k + 2, 1), held)
        return held

    def unpack(packed, k):
        return jnp.where(edge, roll(packed, -(4 * k + 2), 1), 0.0)

    def put_weights(k):
        for a, w in zip(range(-2, 3), weights(vel[k])):
            if k and a:
                at, n = (row3, Y) if k == 1 else (lane3, Z)
                w = jnp.where(at >= n - a if a > 0 else at < -a, 0.0, w)
            wgt[k, a + 2] = w

    def side_of(d):
        return (d + 1) // 2

    def tile(dy):
        return pl.ds(0, Y) if dy == 0 else pl.ds(0 if dy < 0 else Y - 8, 8)

    def spread_x(src, step):
        for c in range(3):
            sx[step, 0, c, 0] = wgt[0, 0, 0] * src[c, 0]
            sx[step, 0, c, 1] = wgt[0, 1, 0] * src[c, 0] + wgt[0, 0, 1] * src[c, 1]
            sx[step, 1, c, 0] = wgt[0, 3, X - 1] * src[c, X - 1] + wgt[0, 4, X - 2] * src[c, X - 2]
            sx[step, 1, c, 1] = wgt[0, 4, X - 1] * src[c, X - 1]
        for s in range(2):
            for t in range(2):
                sxy[step, s, t] = sx[step, s, :, :, (Y - 2) * t:(Y - 2) * t + 2, :]
        szx[step] = pack([
            (c * X + (0 if s else X - 2) + x, sx[step, s, c, x])
            for s in range(2) for c in range(3) for x in range(2)
        ])

    def interior_x(src, step):
        for c in range(3):
            layers = []
            for x in range(X):
                total = None
                for a in range(-2, 3):
                    if 0 <= x - a < X:
                        term = wgt[0, a + 2, x - a] * src[c, x - a]
                        total = term if total is None else total + term
                layers.append(total)
            for x in range(X):
                cur[c, x] = layers[x]
        for t in range(2):
            sy[step, t] = cur[:, :, (Y - 2) * t:(Y - 2) * t + 2, :]
        szi[step] = pack([(c * X + x, cur[c, x]) for c in range(3) for x in range(X)])

    def send_x(step):
        diagonal = [
            push(szx.at[step, tile(dy)],
                 rzx.at[step, i, side_of(dz), dy + 1, pl.ds(0, 8 if dy else Y)], (dx, dy, dz))
            for dy in (-1, 1, 0) for dz in both for i, dx in enumerate(xdirs)
        ]
        corner = [
            push(sxy.at[step, side_of(dx), side_of(dy)],
                 rxy.at[step, side_of(dx), side_of(dy)], (dx, dy, 0))
            for dx in both for dy in both
        ]
        face = [
            push(sx.at[step, side_of(dx)], rx.at[step, side_of(dx)], (dx, 0, 0)) for dx in both
        ]
        return diagonal, corner, face

    def send_packs(src, dst):
        return [
            push(src.at[tile(dy)], dst.at[side_of(dz), dy + 1, pl.ds(0, 8 if dy else Y)], (0, dy, dz))
            for dy in (-1, 1, 0) for dz in both
        ]

    def send_rows(src, dst):
        return [push(src.at[side_of(dy)], dst.at[side_of(dy)], (0, dy, 0)) for dy in both]

    put_weights(0)
    spread_x(vort, 0)
    interior_x(vort, 0)
    for t in range(2):
        svy[t] = vel[:, :, (Y - 2) * t:(Y - 2) * t + 2, :]
    svz[...] = pack([(c * X + x, vel[c, x]) for c in range(3) for x in range(X)])
    pl.semaphore_wait(barrier, greeted)

    diagonal, corner, face = send_x(0)
    rows = send_rows(sy.at[0], ry.at[0])
    packs = send_packs(szi.at[0], rzi.at[0])
    vrows = send_rows(svy, rvy)
    vpacks = send_packs(svz, rvz)
    vface = [
        push(vel.at[:, pl.ds((X - 2) * s, 2)], rvx.at[s], (2 * s - 1, 0, 0)) for s in range(2)
    ]
    put_weights(1)
    put_weights(2)

    scale = TIME_STEP / 12.0
    low_lanes = lane % 4 < 2

    def merge(received, dy):
        count = 8 if dy else Y
        return jnp.where(low_lanes[:count], received[1, dy + 1, :count], received[0, dy + 1, :count])

    def stack(received):
        return jnp.concatenate([merge(received, dy) for dy in (1, 0, -1)], axis=0)

    def repeat(packed, k):
        n = 4 * X
        at = lax.broadcasted_iota(jnp.int32, packed.shape, 1)
        full = jnp.zeros(packed.shape, f32)
        for c in range(3):
            full = jnp.where((at >= c * n) & (at < (c + 1) * n), roll(packed, (c - k) * n, 1), full)
        return full

    def slopes_y():
        for c in range(3):
            v = vel[c]
            slope[1, c] = scale * (
                8.0 * (roll(v, -1, 1) - roll(v, 1, 1)) - (roll(v, -2, 1) - roll(v, 2, 1)))
        done(vrows)
        for c in range(3):
            top = vel[c, :, 0:4, :]
            low = rvy[1, c]
            slope[1, c, :, 0:1, :] = scale * (
                8.0 * (top[:, 1:2] - low[:, 1:2]) - (top[:, 2:3] - low[:, 0:1]))
            slope[1, c, :, 1:2, :] = scale * (
                8.0 * (top[:, 2:3] - top[:, 0:1]) - (top[:, 3:4] - low[:, 1:2]))
            end = vel[c, :, Y - 4:Y, :]
            high = rvy[0, c]
            slope[1, c, :, Y - 2:Y - 1, :] = scale * (
                8.0 * (end[:, 3:4] - end[:, 1:2]) - (high[:, 0:1] - end[:, 0:1]))
            slope[1, c, :, Y - 1:Y, :] = scale * (
                8.0 * (high[:, 0:1] - end[:, 2:3]) - (high[:, 1:2] - end[:, 1:2]))
        for s in range(2):
            w = weights(rvy[s, 1])
            wyh[s, 0] = w[3] if s else w[1]
            wyh[s, 1] = w[4] if s else w[0]

    def slopes_z(halo):
        for c in range(3):
            for x in range(X):
                v = vel[c, x]
                h = roll(halo, -(4 * (c * X + x) + 2), 1)

                def at(shift):
                    mask = lane < shift if shift > 0 else lane >= Z + shift
                    return roll(jnp.where(mask, h, v), -shift, 1)

                slope[2, c, x] = scale * (8.0 * (at(1) - at(-1)) - (at(2) - at(-2)))

    def slopes_x():
        done(vface)
        for c in range(3):
            def layer(x):
                if x < 0:
                    return rvx[1, c, x + 2]
                if x >= X:
                    return rvx[0, c, x - X]
                return vel[c, x]
            for x in range(X):
                slope[0, c, x] = scale * (
                    8.0 * (layer(x + 1) - layer(x - 1)) - (layer(x + 2) - layer(x - 2)))

    wy_packed = wz_packed = None
    for step in range(SUBSTEPS):
        if step > 0:
            spread_x(cur, step)
            diagonal, corner, face = send_x(step)
            interior_x(cur, step)
            rows = send_rows(sy.at[step], ry.at[step])
            packs = send_packs(szi.at[step], rzi.at[step])
        if step == 0:
            slopes_y()
        done(rows)
        done(corner)
        for s in range(2):
            ry[step, s, :, 0:2] += rxy[step, 1, s]
            ry[step, s, :, X - 2:X] += rxy[step, 0, s]
        done(face)
        for c in range(3):
            for x in range(2):
                cur[c, x] += rx[step, 1, c, x]
                cur[c, X - 2 + x] += rx[step, 0, c, x]

        for c in range(3):
            v = cur[c]
            keep = wgt[1, 2] * v
            for a in (-2, -1, 1, 2):
                keep = keep + roll(wgt[1, a + 2] * v, a, 1)
            cur[c] = keep
            low, high = ry[step, 1, c], ry[step, 0, c]
            near, far = wyh[1, 0] * low, wyh[1, 1] * low
            cur[c, :, 0:1, :] += near[:, 1:2] + far[:, 0:1]
            cur[c, :, 1:2, :] += far[:, 1:2]
            near, far = wyh[0, 0] * high, wyh[0, 1] * high
            cur[c, :, Y - 1:Y, :] += near[:, 0:1] + far[:, 1:2]
            cur[c, :, Y - 2:Y - 1, :] += far[:, 0:1]
        for c in range(3):
            v = cur[c]
            keep = wgt[2, 2] * v
            for a in (-2, -1, 1, 2):
                keep = keep + roll(wgt[2, a + 2] * v, a, 2)
            cur[c] = keep

        if step == 0:
            done(vpacks)
            vpacked = stack(rvz)
            wy_packed = weights(repeat(vpacked, 1))
            wz_packed = [w[8:8 + Y] for w in weights(repeat(vpacked, 2))]
            slopes_z(vpacked[8:8 + Y])
            slopes_x()

        done(packs)
        done(diagonal)
        halo = stack(rzi.at[step])
        if len(xdirs) == 1:
            halo = halo + stack(rzx.at[step, 0])
        else:
            x_of = (lax.broadcasted_iota(jnp.int32, halo.shape, 1) // 4) % X
            halo = halo + jnp.where(x_of >= X - 2, stack(rzx.at[step, 0]), 0.0)
            halo = halo + jnp.where(x_of < 2, stack(rzx.at[step, 1]), 0.0)
        spread = wy_packed[2] * halo
        for a in (-2, -1, 1, 2):
            spread = spread + roll(wy_packed[a + 2] * halo, a, 0)
        spread = spread[8:8 + Y]
        up = roll(wz_packed[4] * spread, 2, 1) + jnp.where(
            lane % 4 == 2, roll(wz_packed[3] * spread, 1, 1), 0.0)
        down = roll(wz_packed[0] * spread, -2, 1) + jnp.where(
            lane % 4 == 1, roll(wz_packed[1] * spread, -1, 1), 0.0)
        ghosts = jnp.where(low_lanes, down, up)

        final = out if step == SUBSTEPS - 1 else cur
        for x in range(X):
            v = [cur[c, x] + unpack(ghosts, c * X + x) for c in range(3)]
            for i in range(3):
                total = v[i]
                for j in range(3):
                    total = total + v[j] * slope[j, i, x]
                final[i, x] = total


def solution(mesh):
    sizes = [mesh.shape[a] for a in AXES]

    def local(vort, vel):
        _, X, Y, Z = vort.shape
        assert 12 * X <= Z and Y % 8 == 0
        f32 = jnp.float32
        V = pltpu.VMEM
        S = SUBSTEPS
        xdirs = 1 if sizes[0] == 2 else 2
        messages = S * (2 + 2 + 4 + 6 + 6 * xdirs) + 2 + 2 + 6
        return pl.pallas_call(
            functools.partial(body, sizes),
            out_shape=jax.ShapeDtypeStruct(vort.shape, f32),
            in_specs=[pl.BlockSpec(memory_space=pltpu.VMEM)] * 2,
            out_specs=pl.BlockSpec(memory_space=pltpu.VMEM),
            scratch_shapes=[
                V((3, 5, X, Y, Z), f32),
                V((3, 3, X, Y, Z), f32),
                V((3, X, Y, Z), f32),
                V((S, 2, 3, 2, Y, Z), f32),
                V((S, 2, 3, 2, Y, Z), f32),
                V((S, 2, 3, X, 2, Z), f32),
                V((S, 2, 3, X, 2, Z), f32),
                V((S, 2, 2, 3, 2, 2, Z), f32),
                V((S, 2, 2, 3, 2, 2, Z), f32),
                V((S, Y, Z), f32),
                V((S, 2, 3, Y, Z), f32),
                V((S, Y, Z), f32),
                V((S, xdirs, 2, 3, Y, Z), f32),
                V((2, 3, 2, Y, Z), f32),
                V((2, 3, X, 2, Z), f32),
                V((2, 3, X, 2, Z), f32),
                V((Y, Z), f32),
                V((2, 3, Y, Z), f32),
                V((2, 2, X, 2, Z), f32),
                pltpu.SemaphoreType.DMA((messages,)),
                pltpu.SemaphoreType.DMA((messages,)),
            ],
            compiler_params=pltpu.CompilerParams(collective_id=0, has_side_effects=True),
        )(vort, vel)

    placed = P(None, *AXES)
    return jax.shard_map(
        local, mesh=mesh, in_specs=(placed, placed), out_specs=placed, check_vma=False
    )
```

time: 29.9 us -> 24.5 us (0.82)
  Pallas kernels: 28.1 us -> 22.7 us
    pallas_call x1, Pallas kernels: 28.1 us -> 22.7 us  [local(): pl.pallas_call(functools.partial(body, sizes), out_shape=jax.ShapeDtypeSt...]
where the time goes in v2:
time: 24.5 us; the launch traced here: 24.3 us
  Pallas kernels  22.7 us (93%)
  local copies, waits for them, and re-layouts  1.62 us (7%)
    pallas_call x1, Pallas kernels, local(): pl.pallas_call(functools.partial(body, sizes), out_shape=jax.ShapeDtypeSt...  22.7 us
    unnamed x1, local copies, waits for them, and re-layouts  1.62 us

profile of v2, /device:TPU:0, one launch (start us, length us, event | category | flops | bytes accessed | tf_op | source)
XLA Modules:
  0.0 24.3 jit_solution(12284960737956131116)
XLA Ops:
  0.0 22.7 %shard_map.28 = f32[3,8,16,128]{3,2,1,0:T(8,128)} custom-call(f32[3,8,16,128]{3,2,1,0:T(8,128)} %vort.1, f32[3,8,16,128]{3,2,1,0:T(8,128)} %vel.1), custom_call_target="tpu_custom_call" | custom-call | tf_op jit(solution)/shard_map/pallas_call | solution.py:337
  22.7 1.6 %copy.4 = f32[3,8,16,128]{3,2,1,0:T(8,128)} copy(f32[3,8,16,128]{3,2,1,0:T(8,128)} %shard_map.28) | data formatting | bytes 393216

commit v3 on v2

--- a/solution.py
+++ b/solution.py
@@ -36,8 +36,8 @@
 
 
 def body(
-    sizes, vort, vel, out, wgt, slope, cur, sx, rx, sy, ry, sxy, rxy, szi, rzi, szx, rzx,
-    rvx, svy, rvy, svz, rvz, wyh, send_sem, recv_sem,
+    sizes, vort_in, vel_in, out, vort, vel, wgt, slope, cur, sx, rx, sy, ry, sxy, rxy, szi, rzi, szx, rzx,
+    rvx, svy, rvy, svz, rvz, wyh, send_sem, recv_sem, load_sem,
 ):
     _, X, Y, Z = vort.shape
     here = [lax.axis_index(a) for a in AXES]
@@ -76,6 +76,12 @@
                     pl.semaphore_signal(
                         barrier, inc=1, device_id=device((dx, dy, dz)), device_id_type=MESH)
                     greeted += 1
+    loads = [
+        pltpu.make_async_copy(src, dst, load_sem.at[i])
+        for i, (src, dst) in enumerate(((vel_in, vel), (vort_in, vort)))
+    ]
+    for load in loads:
+        load.start()
 
     lane = lax.broadcasted_iota(jnp.int32, (Y, Z), 1)
     lane3 = lax.broadcasted_iota(jnp.int32, (X, Y, Z), 2)
@@ -159,12 +165,25 @@
     def send_rows(src, dst):
         return [push(src.at[side_of(dy)], dst.at[side_of(dy)], (0, dy, 0)) for dy in both]
 
+    loads[0].wait()
     put_weights(0)
+    loads[1].wait()
     spread_x(vort, 0)
     interior_x(vort, 0)
     for t in range(2):
         svy[t] = vel[:, :, (Y - 2) * t:(Y - 2) * t + 2, :]
     svz[...] = pack([(c * X + x, vel[c, x]) for c in range(3) for x in range(X)])
+    put_weights(1)
+    put_weights(2)
+    scale = TIME_STEP / 12.0
+    for c in range(3):
+        v = vel[c]
+        slope[1, c] = scale * (
+            8.0 * (roll(v, -1, 1) - roll(v, 1, 1)) - (roll(v, -2, 1) - roll(v, 2, 1)))
+    for c in range(3):
+        for x in range(2, X - 2):
+            slope[0, c, x] = scale * (
+                8.0 * (vel[c, x + 1] - vel[c, x - 1]) - (vel[c, x + 2] - vel[c, x - 2]))
     pl.semaphore_wait(barrier, greeted)
 
     diagonal, corner, face = send_x(0)
@@ -175,10 +194,6 @@
     vface = [
         push(vel.at[:, pl.ds((X - 2) * s, 2)], rvx.at[s], (2 * s - 1, 0, 0)) for s in range(2)
     ]
-    put_weights(1)
-    put_weights(2)
-
-    scale = TIME_STEP / 12.0
     low_lanes = lane % 4 < 2
 
     def merge(received, dy):
@@ -197,10 +212,6 @@
         return full
 
     def slopes_y():
-        for c in range(3):
-            v = vel[c]
-            slope[1, c] = scale * (
-                8.0 * (roll(v, -1, 1) - roll(v, 1, 1)) - (roll(v, -2, 1) - roll(v, 2, 1)))
         done(vrows)
         for c in range(3):
             top = vel[c, :, 0:4, :]
@@ -241,7 +252,7 @@
                 if x >= X:
                     return rvx[0, c, x - X]
                 return vel[c, x]
-            for x in range(X):
+            for x in (0, 1, X - 2, X - 1):
                 slope[0, c, x] = scale * (
                     8.0 * (layer(x + 1) - layer(x - 1)) - (layer(x + 2) - layer(x - 2)))
 
@@ -337,9 +348,11 @@
         return pl.pallas_call(
             functools.partial(body, sizes),
             out_shape=jax.ShapeDtypeStruct(vort.shape, f32),
-            in_specs=[pl.BlockSpec(memory_space=pltpu.VMEM)] * 2,
+            in_specs=[pl.BlockSpec(memory_space=pltpu.MemorySpace.HBM)] * 2,
             out_specs=pl.BlockSpec(memory_space=pltpu.VMEM),
             scratch_shapes=[
+                V((3, X, Y, Z), f32),
+                V((3, X, Y, Z), f32),
                 V((3, 5, X, Y, Z), f32),
                 V((3, 3, X, Y, Z), f32),
                 V((3, X, Y, Z), f32),
@@ -361,6 +374,7 @@
                 V((2, 2, X, 2, Z), f32),
                 pltpu.SemaphoreType.DMA((messages,)),
                 pltpu.SemaphoreType.DMA((messages,)),
+                pltpu.SemaphoreType.DMA((2,)),
             ],
             compiler_params=pltpu.CompilerParams(collective_id=0, has_side_effects=True),
         )(vort, vel)

time: 24.5 us -> 23.4 us (0.955)
  Pallas kernels: 22.7 us -> 21.7 us
    pallas_call x1, Pallas kernels: 22.7 us -> 21.7 us  [local(): pl.pallas_call(functools.partial(body, sizes), out_shape=jax.ShapeDtypeSt...]
where the time goes in v3:
time: 23.4 us; the launch traced here: 23.3 us
  Pallas kernels  21.7 us (93%)
  local copies, waits for them, and re-layouts  1.62 us (7%)
    pallas_call x1, Pallas kernels, local(): pl.pallas_call(functools.partial(body, sizes), out_shape=jax.ShapeDtypeSt...  21.7 us
    unnamed x1, local copies, waits for them, and re-layouts  1.62 us

profile of v3, /device:TPU:0, one launch (start us, length us, event | category | flops | bytes accessed | tf_op | source)
XLA Modules:
  0.0 23.3 jit_solution(7197443397451408264)
XLA Ops:
  0.0 21.7 %shard_map.28 = f32[3,8,16,128]{3,2,1,0:T(8,128)} custom-call(f32[3,8,16,128]{3,2,1,0:T(8,128)} %vort_in.1, f32[3,8,16,128]{3,2,1,0:T(8,128)} %vel_in.1), custom_call_target="tpu_custom_call" | custom-call | tf_op jit(solution)/shard_map/pallas_call | solution.py:348
  21.7 1.6 %copy.4 = f32[3,8,16,128]{3,2,1,0:T(8,128)} copy(f32[3,8,16,128]{3,2,1,0:T(8,128)} %shard_map.28) | data formatting | bytes 393216

commit v4 on v3

--- a/solution.py
+++ b/solution.py
@@ -256,54 +256,52 @@
                 slope[0, c, x] = scale * (
                     8.0 * (layer(x + 1) - layer(x - 1)) - (layer(x + 2) - layer(x - 2)))
 
+    def remesh_yz(step, lo, hi):
+        at = slice(lo, hi)
+        for c in range(3):
+            v = cur[c, at]
+            keep = wgt[1, 2, at] * v
+            for a in (-2, -1, 1, 2):
+                keep = keep + roll(wgt[1, a + 2, at] * v, a, 1)
+            cur[c, at] = keep
+            low, high = ry[step, 1, c, at], ry[step, 0, c, at]
+            near, far = wyh[1, 0, at] * low, wyh[1, 1, at] * low
+            cur[c, at, 0:1, :] += near[:, 1:2] + far[:, 0:1]
+            cur[c, at, 1:2, :] += far[:, 1:2]
+            near, far = wyh[0, 0, at] * high, wyh[0, 1, at] * high
+            cur[c, at, Y - 1:Y, :] += near[:, 0:1] + far[:, 1:2]
+            cur[c, at, Y - 2:Y - 1, :] += far[:, 0:1]
+        for c in range(3):
+            v = cur[c, at]
+            keep = wgt[2, 2, at] * v
+            for a in (-2, -1, 1, 2):
+                keep = keep + roll(wgt[2, a + 2, at] * v, a, 2)
+            cur[c, at] = keep
+
+    borders = (0, 1, X - 2, X - 1)
     wy_packed = wz_packed = None
     for step in range(SUBSTEPS):
-        if step > 0:
-            spread_x(cur, step)
-            diagonal, corner, face = send_x(step)
-            interior_x(cur, step)
-            rows = send_rows(sy.at[step], ry.at[step])
-            packs = send_packs(szi.at[step], rzi.at[step])
         if step == 0:
             slopes_y()
         done(rows)
-        done(corner)
-        for s in range(2):
-            ry[step, s, :, 0:2] += rxy[step, 1, s]
-            ry[step, s, :, X - 2:X] += rxy[step, 0, s]
-        done(face)
-        for c in range(3):
-            for x in range(2):
-                cur[c, x] += rx[step, 1, c, x]
-                cur[c, X - 2 + x] += rx[step, 0, c, x]
-
-        for c in range(3):
-            v = cur[c]
-            keep = wgt[1, 2] * v
-            for a in (-2, -1, 1, 2):
-                keep = keep + roll(wgt[1, a + 2] * v, a, 1)
-            cur[c] = keep
-            low, high = ry[step, 1, c], ry[step, 0, c]
-            near, far = wyh[1, 0] * low, wyh[1, 1] * low
-            cur[c, :, 0:1, :] += near[:, 1:2] + far[:, 0:1]
-            cur[c, :, 1:2, :] += far[:, 1:2]
-            near, far = wyh[0, 0] * high, wyh[0, 1] * high
-            cur[c, :, Y - 1:Y, :] += near[:, 0:1] + far[:, 1:2]
-            cur[c, :, Y - 2:Y - 1, :] += far[:, 0:1]
-        for c in range(3):
-            v = cur[c]
-            keep = wgt[2, 2] * v
-            for a in (-2, -1, 1, 2):
-                keep = keep + roll(wgt[2, a + 2] * v, a, 2)
-            cur[c] = keep
-
+        remesh_yz(step, 2, X - 2)
         if step == 0:
             done(vpacks)
             vpacked = stack(rvz)
             wy_packed = weights(repeat(vpacked, 1))
             wz_packed = [w[8:8 + Y] for w in weights(repeat(vpacked, 2))]
             slopes_z(vpacked[8:8 + Y])
-            slopes_x()
+        done(corner)
+        for s in range(2):
+            ry[step, s, :, 0:2] += rxy[step, 1, s]
+            ry[step, s, :, X - 2:X] += rxy[step, 0, s]
+        done(face)
+        for c in range(3):
+            for x in range(2):
+                cur[c, x] += rx[step, 1, c, x]
+                cur[c, X - 2 + x] += rx[step, 0, c, x]
+        remesh_yz(step, 0, 2)
+        remesh_yz(step, X - 2, X)
 
         done(packs)
         done(diagonal)
@@ -323,15 +321,30 @@
         down = roll(wz_packed[0] * spread, -2, 1) + jnp.where(
             lane % 4 == 1, roll(wz_packed[1] * spread, -1, 1), 0.0)
         ghosts = jnp.where(low_lanes, down, up)
+        if step == 0:
+            slopes_x()
 
         final = out if step == SUBSTEPS - 1 else cur
-        for x in range(X):
+
+        def finish(x):
             v = [cur[c, x] + unpack(ghosts, c * X + x) for c in range(3)]
             for i in range(3):
                 total = v[i]
                 for j in range(3):
                     total = total + v[j] * slope[j, i, x]
                 final[i, x] = total
+
+        for x in borders:
+            finish(x)
+        if step < SUBSTEPS - 1:
+            spread_x(cur, step + 1)
+            diagonal, corner, face = send_x(step + 1)
+        for x in range(2, X - 2):
+            finish(x)
+        if step < SUBSTEPS - 1:
+            interior_x(cur, step + 1)
+            rows = send_rows(sy.at[step + 1], ry.at[step + 1])
+            packs = send_packs(szi.at[step + 1], rzi.at[step + 1])
 
 
 def solution(mesh):
@@ -347,7 +360,7 @@
         messages = S * (2 + 2 + 4 + 6 + 6 * xdirs) + 2 + 2 + 6
         return pl.pallas_call(
             functools.partial(body, sizes),
-            out_shape=jax.ShapeDtypeStruct(vort.shape, f32),
+            out_shape=pltpu.MemorySpace.VMEM(vort.shape, f32),
             in_specs=[pl.BlockSpec(memory_space=pltpu.MemorySpace.HBM)] * 2,
             out_specs=pl.BlockSpec(memory_space=pltpu.VMEM),
             scratch_shapes=[

time: 23.4 us -> 21.5 us (0.919)
  Pallas kernels: 21.7 us -> 20.7 us
  local copies, waits for them, and re-layouts: 1.62 us -> 0.68 us
    pallas_call x1, Pallas kernels: 21.7 us -> 20.7 us  [local(): pl.pallas_call(functools.partial(body, sizes), out_shape=pltpu.MemorySpac...]
    unnamed x1, local copies, waits for them, and re-layouts: 1.62 us -> 0.68 us
where the time goes in v4:
time: 21.5 us; the launch traced here: 21.4 us
  Pallas kernels  20.7 us (96%)
  local copies, waits for them, and re-layouts  0.68 us (3%)
    pallas_call x1, Pallas kernels, local(): pl.pallas_call(functools.partial(body, sizes), out_shape=pltpu.MemorySpac...  20.7 us
    unnamed x1, local copies, waits for them, and re-layouts  0.68 us

profile of v4, /device:TPU:0, one launch (start us, length us, event | category | flops | bytes accessed | tf_op | source)
XLA Modules:
  0.0 21.4 jit_solution(2752575308640178779)
XLA Ops:
  0.0 20.7 %shard_map.28 = f32[3,8,16,128]{3,2,1,0:T(8,128)S(1)} custom-call(f32[3,8,16,128]{3,2,1,0:T(8,128)} %vort_in.1, f32[3,8,16,128]{3,2,1,0:T(8,128)} %vel_in.1), custom_call_target="tpu_custom_call" | custom-call | tf_op jit(solution)/shard_map/pallas_call | solution.py:361
  20.7 0.7 %copy.4 = f32[3,8,16,128]{3,2,1,0:T(8,128)} copy(f32[3,8,16,128]{3,2,1,0:T(8,128)S(1)} %shard_map.28) | data formatting | bytes 393216

commit v5 on v4

--- a/solution.py
+++ b/solution.py
@@ -108,7 +108,10 @@
         return (d + 1) // 2
 
     def tile(dy):
-        return pl.ds(0, Y) if dy == 0 else pl.ds(0 if dy < 0 else Y - 8, 8)
+        return pl.ds(0, Y) if dy == 0 else pl.ds(0 if dy < 0 else Y - 2, 2)
+
+    def slot(dy):
+        return pl.ds(0, Y) if dy == 0 else pl.ds(0 if dy < 0 else 6, 2)
 
     def spread_x(src, step):
         for c in range(3):
@@ -143,22 +146,22 @@
     def send_x(step):
         diagonal = [
             push(szx.at[step, tile(dy)],
-                 rzx.at[step, i, side_of(dz), dy + 1, pl.ds(0, 8 if dy else Y)], (dx, dy, dz))
+                 rzx.at[step, i, side_of(dz), dy + 1, slot(dy)], (dx, dy, dz))
             for dy in (-1, 1, 0) for dz in both for i, dx in enumerate(xdirs)
+        ]
+        face = [
+            push(sx.at[step, side_of(dx)], rx.at[step, side_of(dx)], (dx, 0, 0)) for dx in both
         ]
         corner = [
             push(sxy.at[step, side_of(dx), side_of(dy)],
                  rxy.at[step, side_of(dx), side_of(dy)], (dx, dy, 0))
             for dx in both for dy in both
         ]
-        face = [
-            push(sx.at[step, side_of(dx)], rx.at[step, side_of(dx)], (dx, 0, 0)) for dx in both
-        ]
         return diagonal, corner, face
 
     def send_packs(src, dst):
         return [
-            push(src.at[tile(dy)], dst.at[side_of(dz), dy + 1, pl.ds(0, 8 if dy else Y)], (0, dy, dz))
+            push(src.at[tile(dy)], dst.at[side_of(dz), dy + 1, slot(dy)], (0, dy, dz))
             for dy in (-1, 1, 0) for dz in both
         ]
 

time: 21.5 us -> 20.9 us (0.972)
  Pallas kernels: 20.7 us -> 20.1 us
    pallas_call x1, Pallas kernels: 20.7 us -> 20.1 us  [local(): pl.pallas_call(functools.partial(body, sizes), out_shape=pltpu.MemorySpac...]
where the time goes in v5:
time: 20.9 us; the launch traced here: 20.7 us
  Pallas kernels  20.1 us (96%)
  local copies, waits for them, and re-layouts  0.68 us (3%)
    pallas_call x1, Pallas kernels, local(): pl.pallas_call(functools.partial(body, sizes), out_shape=pltpu.MemorySpac...  20.1 us
    unnamed x1, local copies, waits for them, and re-layouts  0.68 us

profile of v5, /device:TPU:0, one launch (start us, length us, event | category | flops | bytes accessed | tf_op | source)
XLA Modules:
  0.0 20.7 jit_solution(7664464270445199480)
XLA Ops:
  0.0 20.1 %shard_map.28 = f32[3,8,16,128]{3,2,1,0:T(8,128)S(1)} custom-call(f32[3,8,16,128]{3,2,1,0:T(8,128)} %vort_in.1, f32[3,8,16,128]{3,2,1,0:T(8,128)} %vel_in.1), custom_call_target="tpu_custom_call" | custom-call | tf_op jit(solution)/shard_map/pallas_call | solution.py:364
  20.1 0.7 %copy.4 = f32[3,8,16,128]{3,2,1,0:T(8,128)} copy(f32[3,8,16,128]{3,2,1,0:T(8,128)S(1)} %shard_map.28) | data formatting | bytes 393216

commit v6 on v5

--- a/solution.py
+++ b/solution.py
@@ -288,23 +288,24 @@
             slopes_y()
         done(rows)
         remesh_yz(step, 2, X - 2)
+        done(corner)
+        for s in range(2):
+            ry[step, s, :, 0:2] += rxy[step, 1, s]
+            ry[step, s, :, X - 2:X] += rxy[step, 0, s]
+        done(face)
+        for c in range(3):
+            for x in range(2):
+                cur[c, x] += rx[step, 1, c, x]
+                cur[c, X - 2 + x] += rx[step, 0, c, x]
+        remesh_yz(step, 0, 2)
+        remesh_yz(step, X - 2, X)
+
         if step == 0:
             done(vpacks)
             vpacked = stack(rvz)
             wy_packed = weights(repeat(vpacked, 1))
             wz_packed = [w[8:8 + Y] for w in weights(repeat(vpacked, 2))]
             slopes_z(vpacked[8:8 + Y])
-        done(corner)
-        for s in range(2):
-            ry[step, s, :, 0:2] += rxy[step, 1, s]
-            ry[step, s, :, X - 2:X] += rxy[step, 0, s]
-        done(face)
-        for c in range(3):
-            for x in range(2):
-                cur[c, x] += rx[step, 1, c, x]
-                cur[c, X - 2 + x] += rx[step, 0, c, x]
-        remesh_yz(step, 0, 2)
-        remesh_yz(step, X - 2, X)
 
         done(packs)
         done(diagonal)

time: 20.9 us -> 21 us (level)
  no operation moved by 1% of the time
where the time goes in v6:
time: 21 us; the launch traced here: 20.8 us
  Pallas kernels  20.1 us (96%)
  local copies, waits for them, and re-layouts  0.68 us (3%)
    pallas_call x1, Pallas kernels, local(): pl.pallas_call(functools.partial(body, sizes), out_shape=pltpu.MemorySpac...  20.1 us
    unnamed x1, local copies, waits for them, and re-layouts  0.68 us

profile of v6, /device:TPU:0, one launch (start us, length us, event | category | flops | bytes accessed | tf_op | source)
XLA Modules:
  0.0 20.8 jit_solution(17538574055781525423)
XLA Ops:
  0.0 20.1 %shard_map.28 = f32[3,8,16,128]{3,2,1,0:T(8,128)S(1)} custom-call(f32[3,8,16,128]{3,2,1,0:T(8,128)} %vort_in.1, f32[3,8,16,128]{3,2,1,0:T(8,128)} %vel_in.1), custom_call_target="tpu_custom_call" | custom-call | tf_op jit(solution)/shard_map/pallas_call | solution.py:365
  20.2 0.7 %copy.4 = f32[3,8,16,128]{3,2,1,0:T(8,128)} copy(f32[3,8,16,128]{3,2,1,0:T(8,128)S(1)} %shard_map.28) | data formatting | bytes 393216
